TPU v7x, 32 devices: a whole 2x2x4 slice. The times are simulated.
32 devices in a mesh: dp: 4 (over y, x), expert: 4 (over z), tensor: 2 (over core).
Axes of the slice: x: 2, y: 2, z: 4, core: 2. Of those that a mesh axis runs over, the one named last changes fastest.
Arguments:
- tokens: bfloat16 [2048, 2560], P(('dp', 'expert')), may hold values from -6 to 6
- norm_gain: float32 [2560], replicated, may hold values from 0.5 to 1.5
- expert_ids: int32 [2048, 6], P(('dp', 'expert')), may hold values from 0 to 31, all different within a row; in each aligned block of 128 rows (0 to 127, 128 to 255, ...) at most 48 rows name the same one
- route_weights: int32 [2048, 6], P(('dp', 'expert')), may hold values from 1 to 64
- w_gate: bfloat16 [32, 2560, 768], P('expert', None, 'tensor'), may hold values from -0.125 to 0.125
- w_up: bfloat16 [32, 2560, 768], P('expert', None, 'tensor'), may hold values from -0.125 to 0.125
- w_down: bfloat16 [32, 768, 2560], P('expert', 'tensor'), may hold values from -0.21875 to 0.21875
- shared_gate: bfloat16 [2560, 2048], P(None, ('dp', 'tensor')), may hold values from -0.125 to 0.125
- shared_up: bfloat16 [2560, 2048], P(None, ('dp', 'tensor')), may hold values from -0.125 to 0.125
- shared_down: bfloat16 [2048, 2560], P(('dp', 'tensor')), may hold values from -0.125 to 0.125
Outputs:
- mixed: bfloat16 [2048, 2560], P(('dp', 'expert'), 'tensor')
Inputs may be any that keep to these rules, and one draw needn't show every extreme that they name: `expert_ids`: each row names 6 different experts. In each aligned block of 128 rows (the rows of one index of dp+expert) no expert is named by more than 48 rows, a bound that some blocks reach.
All inputs are finite; a program needn't handle non-finite values.
Results may differ from a plain program's by a relative error of at most 0.011.
Values may be sent and summed in bfloat16 or wider, within the bound.
A program may use at most 128 MiB of HBM per device.

v0:
```python
import jax
import jax.numpy as jnp
from jax import lax
from jax.sharding import PartitionSpec as P

EPSILON = 1e-06
LANES = 128


def normalize(tokens, norm_gain):
    values = tokens.astype(jnp.float32)
    inverse = lax.rsqrt(jnp.mean(values * values, axis=1, keepdims=True) + EPSILON)
    return (values * inverse * norm_gain[None, :]).astype(jnp.bfloat16)


def by_owner(partial, blocks, width):
    rows = partial.shape[0] // blocks
    parts = partial.shape[1] // width
    split = partial.reshape(blocks, rows, parts, width)
    return split.transpose(0, 2, 1, 3).reshape(blocks * parts * rows, width)


def on_device(
    tokens,
    norm_gain,
    expert_ids,
    route_weights,
    w_gate,
    w_up,
    w_down,
    shared_gate,
    shared_up,
    shared_down,
):
    normed = normalize(tokens, norm_gain)
    rows, width = normed.shape
    owners = lax.axis_size("expert")
    groups = lax.axis_size("dp")
    half = width // lax.axis_size("tensor")
    local = w_gate.shape[0]
    experts = local * owners
    lanes = -(-experts // LANES) * LANES
    match = expert_ids[:, :, None] == jnp.arange(lanes, dtype=jnp.int32)[None, None, :]
    scale = jnp.sum(jnp.where(match, route_weights[:, :, None], 0), axis=1)
    scale = (scale.astype(jnp.float32) / 64.0).astype(jnp.bfloat16)
    sent = jnp.concatenate([normed, scale], axis=1)
    everyone = lax.all_gather(sent, "expert", axis=0, tiled=True)
    routed_rows = everyone[:, :width]
    first = lax.axis_index("expert") * local
    mine = lax.dynamic_slice_in_dim(everyone[:, width:], first, local, 1).astype(jnp.float32)
    hidden = []
    for e in range(local):
        gate = jnp.dot(routed_rows, w_gate[e], preferred_element_type=jnp.float32)
        up = jnp.dot(routed_rows, w_up[e], preferred_element_type=jnp.float32)
        hidden.append((jax.nn.silu(gate) * up * mine[:, e : e + 1]).astype(jnp.bfloat16))
    hidden = jnp.concatenate(hidden, axis=1)
    routed = jnp.dot(hidden, w_down.reshape(-1, width), preferred_element_type=jnp.float32)
    routed = by_owner(routed.astype(jnp.bfloat16), owners, half)
    routed = lax.psum_scatter(routed, ("expert", "tensor"), scatter_dimension=0, tiled=True)
    piece = lax.all_gather(normed, "dp", axis=0, tiled=True)
    gate = jnp.dot(piece, shared_gate, preferred_element_type=jnp.float32)
    up = jnp.dot(piece, shared_up, preferred_element_type=jnp.float32)
    shared = (jax.nn.silu(gate) * up).astype(jnp.bfloat16)
    shared = jnp.dot(shared, shared_down, preferred_element_type=jnp.float32)
    shared = by_owner(shared.astype(jnp.bfloat16), groups, half)
    shared = lax.psum_scatter(shared, ("dp", "tensor"), scatter_dimension=0, tiled=True)
    return (shared.astype(jnp.float32) + routed.astype(jnp.float32)).astype(jnp.bfloat16)


def solution(mesh):
    placed = (
        P(("dp", "expert"), None),
        P(),
        P(("dp", "expert"), None),
        P(("dp", "expert"), None),
        P("expert", None, "tensor"),
        P("expert", None, "tensor"),
        P("expert", "tensor", None),
        P(None, ("dp", "tensor")),
        P(None, ("dp", "tensor")),
        P(("dp", "tensor"), None),
    )
    return jax.shard_map(
        on_device,
        mesh=mesh,
        in_specs=placed,
        out_specs=P(("dp", "expert"), "tensor"),
        check_vma=False,
    )
```

profile of v0, /device:TPU:0, one launch (start us, length us, event | category | flops | bytes accessed | tf_op | source)
XLA Modules:
  0.0 212.0 jit_solution(12565851142378850598)
XLA Ops:
  8.0 2.2 %fusion.50 = bf16[128,2560]{1,0:T(8,128)(2,1)} fusion(bf16[128,2560]{1,0:T(8,128)(2,1)} %param.10, f32[2560]{0:T(1024)} %param.11, f32[128]{0:T(128)S(1)} %add_rsqrt_fusion), kind=kLoop, calls=%fused_computation.54 | loop fusion | flops 1310720 | bytes 1321472 | tf_op jit(solution)/shard_map/convert_element_type | solution.py:13
  10.6 2.1 pad_maximum_fusion
  12.7 39.9 %all-gather.3.cloned.1.call-done = bf16[512,2560]{1,0:T(8,128)(2,1)} async-done(((bf16[128,2560]{1,0:T(8,128)(2,1)}), bf16[512,2560]{1,0:T(8,128)(2,1)}) %all-gather.3.cloned.1.call-update) | async-done | bytes 2621456 | tf_op jit(solution)/shard_map/all_gather | solution.py:60
  52.6 2.6 %fusion.171 = f32[512,256]{1,0:T(8,128)S(1)} fusion(bf16[512,2560]{1,0:T(8,128)(2,1)} %all-gather.3.cloned.1.call-done, bf16[2560,256]{1,0:T(8,128)(2,1)S(1)} %copy-done.5), kind=kOutput, calls=%fused_computation.127 | convolution fusion | flops 671088640 | bytes 4456448 | tf_op jit(solution)/shard_map/dot_general | solution.py:61
  55.2 6.4 %convolution_convert_fusion.1 = bf16[512,2560]{1,0:T(8,128)(2,1)} fusion(bf16[256,2560]{1,0:T(8,128)(2,1)S(1)} %copy-done, bf16[512,2560]{1,0:T(8,128)(2,1)} %all-gather.3.cloned.1.call-done, bf16[2560,256]{1,0:T(8,128)(2,1)} %param.18, f32[512,256]{1,0:T(8,128)S(1)} %fusion.171), kind=kOutput, calls=%fused_computation.1 | convolution fusion | flops 1344274432 | bytes 8388608 | tf_op jit(solution)/shard_map/dot_general | solution.py:64
  61.7 5.5 %reshape.26 = bf16[4,128,2,1280]{3,2,1,0:T(2,128)(2,1)S(1)} reshape(bf16[512,2560]{1,0:T(8,128)(2,1)} %convolution_convert_fusion.1) | data formatting | bytes 5242880 | tf_op jit(solution)/shard_map/reshape | solution.py:19
  67.2 1.9 copy.19
  69.3 41.9 %all-gather.5.cloned.1.call-done = bf16[512,2688]{1,0:T(8,128)(2,1)} async-done(((bf16[128,2688]{1,0:T(8,128)(2,1)}), bf16[512,2688]{1,0:T(8,128)(2,1)}) %all-gather.5.cloned.1.call-update) | async-done | bytes 2752528 | tf_op jit(solution)/shard_map/all_gather | solution.py:47
  113.5 2.9 %fusion.30 = f32[512,384]{0,1:T(8,128)S(1)} fusion(bf16[8,2560,384]{2,1,0:T(8,128)(2,1)} %param.14, bf16[512,2688]{1,0:T(8,128)(2,1)S(1)} %copy-done.2), kind=kOutput, calls=%fused_computation.32 | convolution fusion | flops 1006632960 | bytes 5373952 | tf_op jit(solution)/shard_map/dot_general | solution.py:53
  116.5 2.9 %fusion.26 = f32[512,384]{0,1:T(8,128)S(1)} fusion(bf16[8,2560,384]{2,1,0:T(8,128)(2,1)} %param.14, bf16[512,2688]{1,0:T(8,128)(2,1)S(1)} %copy-done.2), kind=kOutput, calls=%fused_computation.28 | convolution fusion | flops 1006632960 | bytes 5373952 | tf_op jit(solution)/shard_map/dot_general | solution.py:53
  119.4 3.1 %fusion.22 = f32[512,384]{0,1:T(8,128)S(1)} fusion(bf16[8,2560,384]{2,1,0:T(8,128)(2,1)} %param.14, bf16[512,2688]{1,0:T(8,128)(2,1)S(1)} %copy-done.2), kind=kOutput, calls=%fused_computation.24 | convolution fusion | flops 1006632960 | bytes 5373952 | tf_op jit(solution)/shard_map/dot_general | solution.py:53
  129.9 2.0 fusion.144
  131.9 2.0 fusion.138
  134.0 2.3 %fusion.132 = bf16[512,3072]{0,1:T(8,128)(2,1)} fusion(bf16[512,3072]{0,1:T(8,128)(2,1)} %fusion.138, bf16[8,2560,384]{2,1,0:T(8,128)(2,1)S(1)} %bitcast.131, f32[512,384]{0,1:T(8,128)S(1)} %fusion.22, f32[512]{0:T(512)S(1)} %get-tuple-element.10, bf16[512,2688]{1,0:T(8,128)(2,1)S(1)} %copy-done.2), kind=kOutput, calls=%fused_computation.82 | convolution fusion | flops 1008009216 | bytes 5769216 | tf_op jit(solution)/shard_map/dot_general | solution.py:54
  136.3 2.1 fusion.126
  138.3 2.0 fusion.120
  141.6 2.1 fusion.114
  143.7 2.0 fusion.108
  145.7 2.1 fusion.102
  147.8 13.0 %convolution_convert_fusion = bf16[512,2560]{1,0:T(8,128)(2,1)S(1)} fusion(bf16[512,3072]{0,1:T(8,128)(2,1)} %fusion.102, bf16[3072,2560]{1,0:T(8,128)(2,1)} %bitcast.132), kind=kOutput, calls=%fused_computation | convolution fusion | flops 8054374400 | bytes 21495808 | tf_op jit(solution)/shard_map/dot_general | solution.py:57
  160.8 2.2 %reshape.29 = bf16[4,128,2,1280]{3,2,1,0:T(2,128)(2,1)} reshape(bf16[512,2560]{1,0:T(8,128)(2,1)S(1)} %convolution_convert_fusion) | data formatting | bytes 5242880 | tf_op jit(solution)/shard_map/reshape | solution.py:19
  163.0 3.7 %copy.20 = bf16[4,2,128,1280]{3,2,1,0:T(8,128)(2,1)} copy(bf16[4,2,128,1280]{3,1,2,0:T(2,128)(2,1)} %bitcast.127) | data formatting | bytes 5242880 | tf_op jit(solution)/shard_map/transpose | solution.py:20
  166.8 36.8 %reduce-scatter.5.cloned.1.call-done = bf16[128,1280]{1,0:T(8,128)(2,1)} async-done(((bf16[1024,1280]{1,0:T(8,128)(2,1)}), bf16[128,1280]{1,0:T(8,128)(2,1)}) %reduce-scatter.5.cloned.1.call-update) | async-done | bytes 327696 | tf_op jit(solution)/shard_map/reduce_scatter | solution.py:59
  203.6 1.9 add_convert_fusion
  (51 shorter events, 13.0 us)
Async XLA Ops:
  6.5 48.7 %copy-start = (bf16[256,2560]{1,0:T(8,128)(2,1)S(1)}, bf16[256,2560]{1,0:T(8,128)(2,1)}, u32[]{:S(2)}) copy-start(bf16[256,2560]{1,0:T(8,128)(2,1)} %param.19) | copy-start | bytes 3932164
  6.5 3.8 %copy-start.4 = (s32[128,6]{0,1:T(8,128)S(1)}, s32[128,6]{0,1:T(8,128)}, u32[]{:S(2)}) copy-start(s32[128,6]{0,1:T(8,128)} %param.12) | copy-start | bytes 9220
  6.5 3.8 %copy-start.3 = (s32[128,6]{0,1:T(8,128)S(1)}, s32[128,6]{0,1:T(8,128)}, u32[]{:S(2)}) copy-start(s32[128,6]{0,1:T(8,128)} %param.13) | copy-start | bytes 9220
  6.5 46.1 %copy-start.5 = (bf16[2560,256]{1,0:T(8,128)(2,1)S(1)}, bf16[2560,256]{1,0:T(8,128)(2,1)}, u32[]{:S(2)}) copy-start(bf16[2560,256]{1,0:T(8,128)(2,1)} %param.17) | copy-start | bytes 3932164
  6.5 46.1 %all-gather.3.cloned.1.call-start = ((), (), s32[]{:S(2)}) async-start(), calls=%async_computation.2 | async-start | bytes 3276800 | tf_op jit(solution)/shard_map/all_gather | solution.py:60
  10.3 100.9 %all-gather.5.cloned.1.call-start = ((), (), s32[]{:S(2)}) async-start(), calls=%async_computation.4 | async-start | bytes 3440640 | tf_op jit(solution)/shard_map/all_gather | solution.py:47
  12.7 154.1 %reduce-scatter.3.cloned.1.call-start = ((), (), s32[]{:S(2)}) async-start(), calls=%async_computation.3 | async-start | bytes 2949120 | tf_op jit(solution)/shard_map/reduce_scatter | solution.py:66
  69.1 134.5 %reduce-scatter.5.cloned.1.call-start = ((), (), s32[]{:S(2)}) async-start(), calls=%async_computation.5 | async-start | bytes 2949120 | tf_op jit(solution)/shard_map/reduce_scatter | solution.py:59
  111.2 2.3 %copy-start.2 = (bf16[512,2688]{1,0:T(8,128)(2,1)S(1)}, bf16[512,2688]{1,0:T(8,128)(2,1)}, u32[]{:S(2)}) copy-start(bf16[512,2688]{1,0:T(8,128)(2,1)} %all-gather.5.cloned.1.call-done) | copy-start | bytes 8257540
  113.5 9.0 %slice-start = ((s8[15728640]{0:T(1024)(128)(4,1)}), s8[4194304]{0:T(1024)(128)(4,1)S(1)}, s32[]{:S(2)}) async-start(s8[15728640]{0:T(1024)(128)(4,1)} %bitcast.128), calls=%async_computation.6 | async-start | bytes 8388608
  113.5 9.0 %slice-start.1 = ((s8[15728640]{0:T(1024)(128)(4,1)}), s8[4194304]{0:T(1024)(128)(4,1)S(1)}, s32[]{:S(2)}) async-start(s8[15728640]{0:T(1024)(128)(4,1)} %bitcast.128), calls=%async_computation.7 | async-start | bytes 8388608
  116.4 6.1 %slice-start.2 = ((s8[15728640]{0:T(1024)(128)(4,1)}), s8[4194304]{0:T(1024)(128)(4,1)S(1)}, s32[]{:S(2)}) async-start(s8[15728640]{0:T(1024)(128)(4,1)} %bitcast.128), calls=%async_computation.8 | async-start | bytes 8388608
  119.4 3.1 %slice-start.3 = ((s8[15728640]{0:T(1024)(128)(4,1)}), s8[3145728]{0:T(1024)(128)(4,1)S(1)}, s32[]{:S(2)}) async-start(s8[15728640]{0:T(1024)(128)(4,1)} %bitcast.128), calls=%async_computation.9 | async-start | bytes 6291456
  123.8 3.8 %slice-start.4 = ((s8[15728640]{0:T(1024)(128)(4,1)}), s8[4194304]{0:T(1024)(128)(4,1)S(1)}, s32[]{:S(2)}) async-start(s8[15728640]{0:T(1024)(128)(4,1)} %bitcast.130), calls=%async_computation.10 | async-start | bytes 8388608
  123.8 3.8 %slice-start.5 = ((s8[15728640]{0:T(1024)(128)(4,1)}), s8[4194304]{0:T(1024)(128)(4,1)S(1)}, s32[]{:S(2)}) async-start(s8[15728640]{0:T(1024)(128)(4,1)} %bitcast.130), calls=%async_computation.11 | async-start | bytes 8388608
  125.0 4.0 %slice-start.6 = ((s8[15728640]{0:T(1024)(128)(4,1)}), s8[4194304]{0:T(1024)(128)(4,1)S(1)}, s32[]{:S(2)}) async-start(s8[15728640]{0:T(1024)(128)(4,1)} %bitcast.130), calls=%async_computation.12 | async-start | bytes 8388608
  126.3 3.6 %slice-start.7 = ((s8[15728640]{0:T(1024)(128)(4,1)}), s8[3145728]{0:T(1024)(128)(4,1)S(1)}, s32[]{:S(2)}) async-start(s8[15728640]{0:T(1024)(128)(4,1)} %bitcast.130), calls=%async_computation.13 | async-start | bytes 6291456
  163.0 42.4 %copy-start.1 = (bf16[256,2560]{1,0:T(8,128)(2,1)S(1)}, bf16[256,2560]{1,0:T(8,128)(2,1)}, u32[]{:S(2)}) copy-start(bf16[256,2560]{1,0:T(8,128)(2,1)} %param.19) | copy-start | bytes 3932164
Sparse Core Ops, SparseCore 0:
  10.4 42.2 all-gather.2
  54.2 56.9 all-gather.4
  114.5 42.2 reduce-scatter.2
  166.8 36.6 reduce-scatter.4
where the time goes:
time: 212 us
  waiting for transfers between devices  119 us (56%)
  matrix products  53.8 us (25%)
  local copies, waits for them, and re-layouts  17.9 us (8%)
  between operations  13.4 us (6%)
  other arithmetic  7.95 us (4%)
    all_gather x1, waiting for transfers between devices, on_device(): everyone = lax.all_gather(sent, 'expert', axis=0, tiled=True)  41.9 us
    all_gather x1, waiting for transfers between devices, on_device(): piece = lax.all_gather(normed, 'dp', axis=0, tiled=True)  39.9 us
    reduce_scatter x1, waiting for transfers between devices, on_device(): lax.psum_scatter(routed, ('expert', 'tensor'), scatter_dimension=0, tiled...  36.8 us
    dot_general x8, matrix products, on_device(): up = jnp.dot(routed_rows, w_up[e], preferred_element_type=jnp.float32)  16.7 us
    dot_general x8, matrix products, on_device(): gate = jnp.dot(routed_rows, w_gate[e], preferred_element_type=jnp.float32)  15.1 us
    dot_general x1, matrix products, on_device(): jnp.dot(hidden, w_down.reshape(-1, width), preferred_element_type=jnp.flo...  13 us
    reshape x2, local copies, waits for them, and re-layouts, by_owner(): split = partial.reshape(blocks, rows, parts, width)  7.73 us
    dot_general x1, matrix products, on_device(): shared = jnp.dot(shared, shared_down, preferred_element_type=jnp.float32)  6.44 us
  transfers between devices with their start and end apart: 4, of which 3 were waited for; matrix products, arithmetic and copies ran while one was open for 34% of the time, Pallas kernels for 0%

commit v1 on v0

--- a/solution.py
+++ b/solution.py
@@ -44,7 +44,14 @@
     scale = jnp.sum(jnp.where(match, route_weights[:, :, None], 0), axis=1)
     scale = (scale.astype(jnp.float32) / 64.0).astype(jnp.bfloat16)
     sent = jnp.concatenate([normed, scale], axis=1)
-    everyone = lax.all_gather(sent, "expert", axis=0, tiled=True)
+    ring = [sent]
+    for hop in range(3):
+        ring.append(lax.ppermute(ring[-1], "expert", [(dev, (dev + 1) % 4) for dev in range(4)]))
+    everyone = jnp.roll(
+        jnp.concatenate(ring[::-1], axis=0),
+        (lax.axis_index("expert") + 1) * ring[0].shape[0],
+        axis=0,
+    )
     routed_rows = everyone[:, :width]
     first = lax.axis_index("expert") * local
     mine = lax.dynamic_slice_in_dim(everyone[:, width:], first, local, 1).astype(jnp.float32)

time: 212 us -> 223 us (1.052)
  local copies, waits for them, and re-layouts: 17.9 us -> 25.7 us
  matrix products: 53.8 us -> 57.8 us
  waiting for transfers between devices: 119 us -> 115 us
  starting transfers between devices: 0.34 us -> 3.2 us
    ppermute x0 -> x3, waiting for transfers between devices: none -> 53.4 us  [on_device(): lax.ppermute(ring[-1], 'expert', [(dev, (dev + 1) % 4) for dev in range(4)])]
    reduce_scatter x1, waiting for transfers between devices: 0.02 us -> 45.7 us  [on_device(): lax.psum_scatter(shared, ('dp', 'tensor'), scatter_dimension=0, tiled=True)]
    all_gather x1 -> x0, waiting for transfers between devices: 41.9 us -> none  [on_device(): everyone = lax.all_gather(sent, 'expert', axis=0, tiled=True)]
    all_gather x1, waiting for transfers between devices: 39.9 us -> 0.02 us  [on_device(): piece = lax.all_gather(normed, 'dp', axis=0, tiled=True)]
    reduce_scatter x1, waiting for transfers between devices: 36.8 us -> 15.8 us  [on_device(): lax.psum_scatter(routed, ('expert', 'tensor'), scatter_dimension=0, tiled...]
    reshape x2, local copies, waits for them, and re-layouts: 7.73 us -> 13.3 us  [by_owner(): split = partial.reshape(blocks, rows, parts, width)]
    dot_general x8, matrix products: 15.1 us -> 18.9 us  [on_device(): gate = jnp.dot(routed_rows, w_gate[e], preferred_element_type=jnp.float32)]
    ppermute x0 -> x3, starting transfers between devices: none -> 3.11 us  [on_device(): lax.ppermute(ring[-1], 'expert', [(dev, (dev + 1) % 4) for dev in range(4)])]
  transfers between devices with their start and end apart: 4 -> 6, of which waited for: 3 -> 5; matrix products, arithmetic and copies ran while one was open for 34% -> 37% of each run, Pallas kernels for 0% -> 0%
where the time goes in v1:
time: 223 us
  waiting for transfers between devices  115 us (52%)
  matrix products  57.8 us (26%)
  local copies, waits for them, and re-layouts  25.7 us (12%)
  between operations  15.2 us (7%)
  other arithmetic  5.9 us (3%)
  starting transfers between devices  3.2 us (1%)
    ppermute x3, waiting for transfers between devices, on_device(): lax.ppermute(ring[-1], 'expert', [(dev, (dev + 1) % 4) for dev in range(4)])  53.4 us
    reduce_scatter x1, waiting for transfers between devices, on_device(): lax.psum_scatter(shared, ('dp', 'tensor'), scatter_dimension=0, tiled=True)  45.7 us
    dot_general x8, matrix products, on_device(): gate = jnp.dot(routed_rows, w_gate[e], preferred_element_type=jnp.float32)  18.9 us
    dot_general x8, matrix products, on_device(): up = jnp.dot(routed_rows, w_up[e], preferred_element_type=jnp.float32)  16.3 us
    reduce_scatter x1, waiting for transfers between devices, on_device(): lax.psum_scatter(routed, ('expert', 'tensor'), scatter_dimension=0, tiled...  15.8 us
    dot_general x1, matrix products, on_device(): jnp.dot(hidden, w_down.reshape(-1, width), preferred_element_type=jnp.flo...  13.3 us
    reshape x2, local copies, waits for them, and re-layouts, by_owner(): split = partial.reshape(blocks, rows, parts, width)  13.3 us
    transpose x2, local copies, waits for them, and re-layouts, by_owner(): return split.transpose(0, 2, 1, 3).reshape(blocks * parts * rows, width)  7.3 us
  transfers between devices with their start and end apart: 6, of which 5 were waited for; matrix products, arithmetic and copies ran while one was open for 37% of the time, Pallas kernels for 0%

profile of v1, /device:TPU:0, one launch (start us, length us, event | category | flops | bytes accessed | tf_op | source)
XLA Modules:
  0.0 222.7 jit_solution(3615654647368105661)
XLA Ops:
  11.2 3.1 %collective-permute-start = (bf16[128,2688]{1,0:T(8,128)(2,1)S(1)}, bf16[128,2688]{1,0:T(8,128)(2,1)S(1)}, u32[]{:S(2)}, u32[]{:S(2)}) collective-permute-start(bf16[128,2688]{1,0:T(8,128)(2,1)S(1)} %pad_maximum_fusion), channel_id=1, source_target_pairs={{0,2},{2,4},{4,6},{6,0},{1,3},{3,5},{5,7},{7,1},{8,10},{10,12},{12... | collective-permute-start | bytes 2064392 | tf_op jit(solution)/shard_map/ppermute | solution.py:49
  14.3 17.5 %collective-permute-done = bf16[128,2688]{1,0:T(8,128)(2,1)S(1)} collective-permute-done((bf16[128,2688]{1,0:T(8,128)(2,1)S(1)}, bf16[128,2688]{1,0:T(8,128)(2,1)S(1)}, u32[]{:S(2)}, u32[]{:S(2)}) %collective-permute-start) | collective-permute-done | bytes 688160 | tf_op jit(solution)/shard_map/ppermute | solution.py:49
  31.7 18.4 %collective-permute-done.1 = bf16[128,2688]{1,0:T(8,128)(2,1)S(1)} collective-permute-done((bf16[128,2688]{1,0:T(8,128)(2,1)S(1)}, bf16[128,2688]{1,0:T(8,128)(2,1)S(1)}, u32[]{:S(2)}, u32[]{:S(2)}) %collective-permute-start.1) | collective-permute-done | bytes 688160 | tf_op jit(solution)/shard_map/ppermute | solution.py:49
  50.2 17.5 %collective-permute-done.2 = bf16[128,2688]{1,0:T(8,128)(2,1)} collective-permute-done((bf16[128,2688]{1,0:T(8,128)(2,1)S(1)}, bf16[128,2688]{1,0:T(8,128)(2,1)}, u32[]{:S(2)}, u32[]{:S(2)}) %collective-permute-start.2) | collective-permute-done | bytes 688160 | tf_op jit(solution)/shard_map/ppermute | solution.py:49
  70.8 4.1 %fusion.30 = f32[512,384]{0,1:T(8,128)} fusion(bf16[8,2560,384]{2,1,0:T(8,128)(2,1)} %param.14, bf16[1024,2688]{1,0:T(8,128)(2,1)S(1)} %constant_dynamic-update-slice_fusion, s32[]{:T(128)S(6)} %select_n.22), kind=kOutput, calls=%fused_computation.32 | convolution fusion | flops 1006632960 | bytes 5373956 | tf_op jit(solution)/shard_map/dot_general | solution.py:60
  76.0 2.1 fusion.26
  78.1 2.1 fusion.22
  82.4 2.1 fusion.14
  84.5 2.1 fusion.10
  90.0 2.4 %fusion.57 = bf16[512,3072]{0,1:T(8,128)(2,1)S(1)} fusion(f32[512,384]{0,1:T(8,128)} %fusion.30, f32[512]{0:T(512)S(1)} %get-tuple-element.12, bf16[8,2560,384]{2,1,0:T(8,128)(2,1)S(1)} %bitcast.81, bf16[1024,2688]{1,0:T(8,128)(2,1)S(1)} %constant_dynamic-update-slice_fusion, s32[]{:T(128)S(6)} %select_n.22), kind=kOutput, calls=%fused_computation.72 | convolution fusion | flops 1008009216 | bytes 5769220 | tf_op jit(solution)/shard_map/dot_general | solution.py:61
  92.5 2.6 %fusion.58 = bf16[512,3072]{0,1:T(8,128)(2,1)S(1)} fusion(bf16[512,3072]{0,1:T(8,128)(2,1)S(1)} %fusion.57, f32[512,384]{0,1:T(8,128)} %fusion.26, f32[512]{0:T(512)S(1)} %get-tuple-element.11, bf16[8,2560,384]{2,1,0:T(8,128)(2,1)S(1)} %bitcast.81, bf16[1024,2688]{1,0:T(8,128)(2,1)S(1)} %constant_dynamic-update-slice_fusion, s32[]{:T(128)S(6)} %select_n.22), kind=kOutput, calls=%fused_computation.73 | convolution fusion | flops 1008009216 | bytes 5769220 | tf_op jit(solution)/shard_map/dot_general | solution.py:61
  95.1 2.4 %fusion.59 = bf16[512,3072]{0,1:T(8,128)(2,1)S(1)} fusion(bf16[512,3072]{0,1:T(8,128)(2,1)S(1)} %fusion.58, f32[512,384]{0,1:T(8,128)} %fusion.22, f32[512]{0:T(512)S(1)} %get-tuple-element.10, bf16[8,2560,384]{2,1,0:T(8,128)(2,1)S(1)} %bitcast.81, bf16[1024,2688]{1,0:T(8,128)(2,1)S(1)} %constant_dynamic-update-slice_fusion, s32[]{:T(128)S(6)} %select_n.22), kind=kOutput, calls=%fused_computation.74 | convolution fusion | flops 1008009216 | bytes 5769220 | tf_op jit(solution)/shard_map/dot_general | solution.py:61
  97.5 2.4 %fusion.60 = bf16[512,3072]{0,1:T(8,128)(2,1)S(1)} fusion(bf16[512,3072]{0,1:T(8,128)(2,1)S(1)} %fusion.59, f32[512,384]{0,1:T(8,128)} %fusion.18, f32[512]{0:T(512)S(1)} %get-tuple-element.9, bf16[8,2560,384]{2,1,0:T(8,128)(2,1)S(1)} %bitcast.81, bf16[1024,2688]{1,0:T(8,128)(2,1)S(1)} %constant_dynamic-update-slice_fusion, s32[]{:T(128)S(6)} %select_n.22), kind=kOutput, calls=%fused_computation.75 | convolution fusion | flops 1008009216 | bytes 5769220 | tf_op jit(solution)/shard_map/dot_general | solution.py:61
  100.0 2.1 fusion.2
  102.1 2.5 %fusion.61 = bf16[512,3072]{0,1:T(8,128)(2,1)S(1)} fusion(bf16[512,3072]{0,1:T(8,128)(2,1)S(1)} %fusion.60, f32[512,384]{0,1:T(8,128)} %fusion.14, f32[512]{0:T(512)S(1)} %get-tuple-element.8, bf16[8,2560,384]{2,1,0:T(8,128)(2,1)S(1)} %bitcast.81, bf16[1024,2688]{1,0:T(8,128)(2,1)S(1)} %constant_dynamic-update-slice_fusion, s32[]{:T(128)S(6)} %select_n.22), kind=kOutput, calls=%fused_computation.76 | convolution fusion | flops 1008009216 | bytes 5769220 | tf_op jit(solution)/shard_map/dot_general | solution.py:61
  108.6 13.3 %convolution_convert_fusion = bf16[512,2560]{1,0:T(8,128)(2,1)} fusion(bf16[512,3072]{0,1:T(8,128)(2,1)S(1)} %fusion.64, bf16[3072,2560]{1,0:T(8,128)(2,1)} %bitcast.82), kind=kOutput, calls=%fused_computation | convolution fusion | flops 8054374400 | bytes 21495808 | tf_op jit(solution)/shard_map/dot_general | solution.py:64
  121.9 6.6 %reshape.29 = bf16[4,128,2,1280]{3,2,1,0:T(2,128)(2,1)} reshape(bf16[512,2560]{1,0:T(8,128)(2,1)} %convolution_convert_fusion) | data formatting | bytes 5242880 | tf_op jit(solution)/shard_map/reshape | solution.py:19
  128.6 3.7 %copy.20 = bf16[4,2,128,1280]{3,2,1,0:T(8,128)(2,1)} copy(bf16[4,2,128,1280]{3,1,2,0:T(2,128)(2,1)} %bitcast.78) | data formatting | bytes 5242880 | tf_op jit(solution)/shard_map/transpose | solution.py:20
  132.4 2.6 %fusion.83 = f32[512,256]{1,0:T(8,128)S(1)} fusion(bf16[512,2560]{1,0:T(8,128)(2,1)} %all-gather.2.cloned.1.call-done, bf16[2560,256]{1,0:T(8,128)(2,1)S(1)} %copy-done.4), kind=kOutput, calls=%fused_computation.104 | convolution fusion | flops 671088640 | bytes 4456448 | tf_op jit(solution)/shard_map/dot_general | solution.py:68
  135.0 6.7 %convolution_convert_fusion.1 = bf16[512,2560]{1,0:T(8,128)(2,1)} fusion(bf16[256,2560]{1,0:T(8,128)(2,1)S(1)} %copy-done, bf16[512,2560]{1,0:T(8,128)(2,1)} %all-gather.2.cloned.1.call-done, bf16[2560,256]{1,0:T(8,128)(2,1)} %param.18, f32[512,256]{1,0:T(8,128)S(1)} %fusion.83), kind=kOutput, calls=%fused_computation.1 | convolution fusion | flops 1344274432 | bytes 8388608 | tf_op jit(solution)/shard_map/dot_general | solution.py:71
  141.7 6.7 %reshape.26 = bf16[4,128,2,1280]{3,2,1,0:T(2,128)(2,1)} reshape(bf16[512,2560]{1,0:T(8,128)(2,1)} %convolution_convert_fusion.1) | data formatting | bytes 5242880 | tf_op jit(solution)/shard_map/reshape | solution.py:19
  148.3 3.6 %copy.19 = bf16[4,2,128,1280]{3,2,1,0:T(8,128)(2,1)} copy(bf16[4,2,128,1280]{3,1,2,0:T(2,128)(2,1)} %bitcast.79) | data formatting | bytes 5242880 | tf_op jit(solution)/shard_map/transpose | solution.py:20
  152.0 15.8 %reduce-scatter.5.cloned.1.call-done = bf16[128,1280]{1,0:T(8,128)(2,1)} async-done(((bf16[1024,1280]{1,0:T(8,128)(2,1)}), bf16[128,1280]{1,0:T(8,128)(2,1)}) %reduce-scatter.5.cloned.1.call-update) | async-done | bytes 327696 | tf_op jit(solution)/shard_map/reduce_scatter | solution.py:66
  167.7 45.7 %reduce-scatter.3.cloned.1.call-done = bf16[128,1280]{1,0:T(8,128)(2,1)} async-done(((bf16[1024,1280]{1,0:T(8,128)(2,1)}), bf16[128,1280]{1,0:T(8,128)(2,1)}) %reduce-scatter.3.cloned.1.call-update) | async-done | bytes 327696 | tf_op jit(solution)/shard_map/reduce_scatter | solution.py:73
  (56 shorter events, 19.3 us)
Async XLA Ops:
  7.4 127.6 %copy-start = (bf16[256,2560]{1,0:T(8,128)(2,1)S(1)}, bf16[256,2560]{1,0:T(8,128)(2,1)}, u32[]{:S(2)}) copy-start(bf16[256,2560]{1,0:T(8,128)(2,1)} %param.19) | copy-start | bytes 3932164
  7.4 125.0 %all-gather.2.cloned.1.call-start = ((), (), s32[]{:S(2)}) async-start(), calls=%async_computation.2 | async-start | bytes 3276800 | tf_op jit(solution)/shard_map/all_gather | solution.py:67
  11.1 39.0 %copy-start.1 = (bf16[128,2560]{1,0:T(8,128)(2,1)}, bf16[128,2560]{1,0:T(8,128)(2,1)S(1)}, u32[]{:S(2)}) copy-start(bf16[128,2560]{1,0:T(8,128)(2,1)S(1)} %fusion.50) | copy-start | bytes 1966084
  11.2 20.6 %collective-permute-start = (bf16[128,2688]{1,0:T(8,128)(2,1)S(1)}, bf16[128,2688]{1,0:T(8,128)(2,1)S(1)}, u32[]{:S(2)}, u32[]{:S(2)}) collective-permute-start(bf16[128,2688]{1,0:T(8,128)(2,1)S(1)} %pad_maximum_fusion), channel_id=1, source_target_pairs={{0,2},{2,4},{4,6},{6,0},{1,3},{3,5},{5,7},{7,1},{8,10},{10,12},{12... | collective-permute-start | bytes 2064392 | tf_op jit(solution)/shard_map/ppermute | solution.py:49
  31.7 18.4 %collective-permute-start.1 = (bf16[128,2688]{1,0:T(8,128)(2,1)S(1)}, bf16[128,2688]{1,0:T(8,128)(2,1)S(1)}, u32[]{:S(2)}, u32[]{:S(2)}) collective-permute-start(bf16[128,2688]{1,0:T(8,128)(2,1)S(1)} %collective-permute-done), channel_id=1, source_target_pairs={{0,2},{2,4},{4,6},{6,0},{1,3},{3,5},{5,7},{7,1},{8,10},{10,12},{12... | collective-permute-start | bytes 2064392 | tf_op jit(solution)/shard_map/ppermute | solution.py:49
  50.1 17.6 %collective-permute-start.2 = (bf16[128,2688]{1,0:T(8,128)(2,1)S(1)}, bf16[128,2688]{1,0:T(8,128)(2,1)}, u32[]{:S(2)}, u32[]{:S(2)}) collective-permute-start(bf16[128,2688]{1,0:T(8,128)(2,1)S(1)} %collective-permute-done.1), channel_id=1, source_target_pairs={{0,2},{2,4},{4,6},{6,0},{1,3},{3,5},{5,7},{7,1},{8,10},{10,12},{12... | collective-permute-start | bytes 2064392 | tf_op jit(solution)/shard_map/ppermute | solution.py:49
  50.2 18.9 %copy-start.2 = (bf16[128,2560]{1,0:T(8,128)(2,1)S(1)}, bf16[128,2560]{1,0:T(8,128)(2,1)}, u32[]{:S(2)}) copy-start(bf16[128,2560]{1,0:T(8,128)(2,1)} %copy-done.1) | copy-start | bytes 1966084
  50.2 117.6 %reduce-scatter.5.cloned.1.call-start = ((), (), s32[]{:S(2)}) async-start(), calls=%async_computation.4 | async-start | bytes 2949120 | tf_op jit(solution)/shard_map/reduce_scatter | solution.py:66
  69.2 6.8 %copy-start.3 = (bf16[8,2560,384]{2,1,0:T(8,128)(2,1)S(1)}, bf16[8,2560,384]{2,1,0:T(8,128)(2,1)}, u32[]{:S(2)}) copy-start(bf16[8,2560,384]{2,1,0:T(8,128)(2,1)} %param.14) | copy-start | bytes 47185924
  82.4 7.6 %slice-start = ((s8[15728640]{0:T(1024)(128)(4,1)}), s8[4194304]{0:T(1024)(128)(4,1)S(1)}, s32[]{:S(2)}) async-start(s8[15728640]{0:T(1024)(128)(4,1)} %bitcast.80), calls=%async_computation.5 | async-start | bytes 8388608
  82.4 7.6 %slice-start.1 = ((s8[15728640]{0:T(1024)(128)(4,1)}), s8[4194304]{0:T(1024)(128)(4,1)S(1)}, s32[]{:S(2)}) async-start(s8[15728640]{0:T(1024)(128)(4,1)} %bitcast.80), calls=%async_computation.6 | async-start | bytes 8388608
  84.5 5.5 %slice-start.2 = ((s8[15728640]{0:T(1024)(128)(4,1)}), s8[4194304]{0:T(1024)(128)(4,1)S(1)}, s32[]{:S(2)}) async-start(s8[15728640]{0:T(1024)(128)(4,1)} %bitcast.80), calls=%async_computation.7 | async-start | bytes 8388608
  86.6 3.4 %slice-start.3 = ((s8[15728640]{0:T(1024)(128)(4,1)}), s8[3145728]{0:T(1024)(128)(4,1)S(1)}, s32[]{:S(2)}) async-start(s8[15728640]{0:T(1024)(128)(4,1)} %bitcast.80), calls=%async_computation.8 | async-start | bytes 6291456
  102.1 2.5 %copy-start.6 = (f32[512,384]{0,1:T(8,128)S(1)}, f32[512,384]{0,1:T(8,128)}, u32[]{:S(2)}) copy-start(f32[512,384]{0,1:T(8,128)} %fusion.10) | copy-start | bytes 2359300
  104.6 1.3 copy-start.5
  106.0 1.3 copy-start.7
  128.6 3.8 %copy-start.4 = (bf16[2560,256]{1,0:T(8,128)(2,1)S(1)}, bf16[2560,256]{1,0:T(8,128)(2,1)}, u32[]{:S(2)}) copy-start(bf16[2560,256]{1,0:T(8,128)(2,1)} %param.17) | copy-start | bytes 3932164
  132.3 81.1 %reduce-scatter.3.cloned.1.call-start = ((), (), s32[]{:S(2)}) async-start(), calls=%async_computation.3 | async-start | bytes 2949120 | tf_op jit(solution)/shard_map/reduce_scatter | solution.py:73
Sparse Core Ops, SparseCore 0:
  50.3 40.7 all-gather.1
Sparse Core Ops, SparseCore 1:
  132.4 35.3 reduce-scatter.4
  170.9 42.4 reduce-scatter.2
